TPU v7x, 32 devices: a whole 2x2x4 slice. The times are simulated.
32 devices in a mesh: fsdp: 2 (over x), ctx: 4 (over y, core), tp: 4 (over z).
Axes of the slice: x: 2, y: 2, z: 4, core: 2. Of those that a mesh axis runs over, the one named last changes fastest.
Arguments:
- tokens: bfloat16 [8, 1024, 2048], P('fsdp', 'ctx'), may hold values from -8 to 8
- positions: int32 [8, 1024], P('fsdp', 'ctx'), may hold values from 0 to 383, as said below
- block_ids: int32 [8, 1024], P('fsdp', 'ctx'), may hold values from 0 to 3, as said below
- gain_attend: bfloat16 [2048], P('fsdp'), may hold values from 0.099609375 to 1.8984375
- w_query: bfloat16 [2048, 2048], P('fsdp', 'tp'), may hold values from -0.125 to 0.125
- w_key: bfloat16 [2048, 2048], P('fsdp', 'tp'), may hold values from -0.125 to 0.125
- w_value: bfloat16 [2048, 2048], P('fsdp', 'tp'), may hold values from -0.125 to 0.125
- w_output: bfloat16 [2048, 2048], P('tp', 'fsdp'), may hold values from -1 to 1
- gain_feed: bfloat16 [2048], P('fsdp'), may hold values from 0.099609375 to 1.8984375
- w_gate: bfloat16 [2048, 8192], P('fsdp', 'tp'), may hold values from -0.125 to 0.125
- w_up: bfloat16 [2048, 8192], P('fsdp', 'tp'), may hold values from -0.125 to 0.125
- w_down: bfloat16 [8192, 2048], P('tp', 'fsdp'), may hold values from -0.0625 to 0.0625
- cotangent: bfloat16 [8, 1024, 2048], P('fsdp', 'ctx'), may hold values from -6 to 6
Outputs:
- layer_out: bfloat16 [8, 1024, 2048], P('fsdp', 'ctx')
- grad_input: bfloat16 [8, 1024, 2048], P('fsdp', 'ctx')
- grad_gain_attend: float32 [2048], P(('fsdp', 'ctx'))
- grad_w_query: float32 [2048, 2048], P(('fsdp', 'ctx'), 'tp')
- grad_w_key: float32 [2048, 2048], P(('fsdp', 'ctx'), 'tp')
- grad_w_value: float32 [2048, 2048], P(('fsdp', 'ctx'), 'tp')
- grad_w_output: float32 [2048, 2048], P('tp', ('fsdp', 'ctx'))
- grad_gain_feed: float32 [2048], P(('fsdp', 'ctx'))
- grad_w_gate: float32 [2048, 8192], P(('fsdp', 'ctx'), 'tp')
- grad_w_up: float32 [2048, 8192], P(('fsdp', 'ctx'), 'tp')
- grad_w_down: float32 [8192, 2048], P('tp', ('fsdp', 'ctx'))
- stream_rms: float32 [], replicated
- attend_rms: float32 [], replicated
- feed_rms: float32 [], replicated
Inputs may be any that keep to these rules, and one draw needn't show every extreme that they name: Along each sequence, positions count 0, 1, 2 and so on from the first token of each block, a run of equal block ids. `block_ids`: along each sequence block ids start at 0, never fall and rise by one at each new block.
All inputs are finite; a program needn't handle non-finite values.
Results may differ from a plain program's by a relative error of at most 0.015.
Values may be sent and summed in bfloat16 or wider, within the bound.
A program may use at most 256 MiB of HBM per device.

v0:
```python
import math
import jax
import jax.numpy as jnp
from jax import lax
from jax.sharding import PartitionSpec as P

HD = 128
norm_epsilon = 1e-05
rope_base = 10000.0


def plain_dot(left_side, right_side):
    return jnp.dot(left_side, right_side, preferred_element_type=jnp.float32)


def dot_last(left_side, right_side):
    return lax.dot_general(
        left_side, right_side, (((1,), (1,)), ((), ())), preferred_element_type=jnp.float32
    )


def dot_first(left_side, right_side):
    return lax.dot_general(
        left_side, right_side, (((0,), (0,)), ((), ())), preferred_element_type=jnp.float32
    )


def inverse_rms(values):
    return lax.rsqrt(jnp.mean(values * values, axis=-1, keepdims=True) + norm_epsilon)


def norm_back(grad_norm, values, scale_rows, gain):
    weighted = grad_norm * gain
    inner_mean = jnp.mean(weighted * values, axis=-1, keepdims=True)
    grad_values = (
        scale_rows * weighted - values * (scale_rows * scale_rows * scale_rows) * inner_mean
    )
    grad_gain = jnp.sum(grad_norm * (values * scale_rows), axis=0)
    return (grad_values, grad_gain)


def rope_tables(positions, head_size):
    half_size = head_size // 2
    inverse = jnp.exp(
        jnp.arange(half_size, dtype=jnp.float32) * (-2.0 * math.log(rope_base) / head_size)
    )
    turned = positions.astype(jnp.float32)[..., None, None] * inverse
    return (jnp.cos(turned), jnp.sin(turned))


def rotate(values, cosine, sine_table, direction):
    half_size = values.shape[-1] // 2
    first_half = values[..., :half_size]
    second_half = values[..., half_size:]
    return jnp.concatenate(
        [
            first_half * cosine - direction * (second_half * sine_table),
            direction * (first_half * sine_table) + second_half * cosine,
        ],
        axis=-1,
    )


def spread_rows(piece, ctx_size):
    part = piece.shape[0] // ctx_size
    mine = lax.dynamic_slice_in_dim(piece, lax.axis_index("ctx") * part, part, 0)
    return lax.all_gather(mine, ("fsdp", "ctx"), axis=0, tiled=True)


def spread_columns(piece, ctx_size):
    part = piece.shape[0] // ctx_size
    mine = lax.dynamic_slice_in_dim(piece, lax.axis_index("ctx") * part, part, 0)
    held = lax.all_gather(mine, ("fsdp", "ctx"), axis=0, tiled=True)
    fsdp_size = lax.axis_size("fsdp")
    held = held.reshape(fsdp_size, piece.shape[0], piece.shape[1])
    return jnp.swapaxes(held, 0, 1).reshape(piece.shape[0], fsdp_size * piece.shape[1])


def sum_rows(partial):
    return lax.psum_scatter(
        partial.astype(jnp.bfloat16), "tp", scatter_dimension=0, tiled=True
    ).astype(jnp.float32)


def every_row(rows):
    return lax.all_gather(rows, "tp", axis=0, tiled=True)


def local(
    tokens,
    positions,
    block_ids,
    gain_attend,
    w_query,
    w_key,
    w_value,
    w_output,
    gain_feed,
    w_gate,
    w_up,
    w_down,
    cotangent,
):
    seq_count, block_len, model_width = tokens.shape
    row_count = seq_count * block_len
    ctx_size = lax.axis_size("ctx")
    tp_size = lax.axis_size("tp")
    seq_len = block_len * ctx_size
    heads_here = w_query.shape[1] // HD
    width_here = heads_here * HD
    score_scale = 1.0 / math.sqrt(HD)
    score_shift = math.log(seq_len)
    shape_heads = (seq_count, block_len, heads_here, HD)
    low = jnp.bfloat16
    part_rows = row_count // tp_size
    row_at = lax.axis_index("tp") * part_rows
    token_rows = tokens.reshape(row_count, model_width)
    grad_rows = cotangent.reshape(row_count, model_width)
    token_part = lax.dynamic_slice_in_dim(token_rows, row_at, part_rows, 0).astype(jnp.float32)
    cotangent_part = lax.dynamic_slice_in_dim(grad_rows, row_at, part_rows, 0).astype(jnp.float32)
    qkv_full = spread_rows(jnp.concatenate([w_query, w_key, w_value], axis=1), ctx_size)
    gains = lax.all_gather(jnp.stack([gain_attend, gain_feed]), "fsdp", axis=1, tiled=True)
    gain_one = gains[0].astype(jnp.float32)
    gain_two = gains[1].astype(jnp.float32)
    output_full = spread_columns(w_output, ctx_size)
    gate_full = spread_rows(w_gate, ctx_size)
    up_full = spread_rows(w_up, ctx_size)
    down_full = spread_columns(w_down, ctx_size)
    stream = token_rows.astype(jnp.float32)
    scale_one = inverse_rms(stream)
    normed_one = (stream * scale_one * gain_one).astype(low)
    projected = plain_dot(normed_one, qkv_full)
    queries = projected[:, :width_here]
    key_proj = projected[:, width_here : 2 * width_here]
    values = projected[:, 2 * width_here :].astype(low)
    cosine, sine_table = rope_tables(positions, HD)
    query_rot = rotate(queries.reshape(shape_heads), cosine, sine_table, 1.0).astype(low)
    key_rot = rotate(key_proj.reshape(shape_heads), cosine, sine_table, 1.0).astype(low)
    key_value = lax.all_gather(
        jnp.concatenate(
            [
                key_rot.reshape(seq_count, block_len, width_here),
                values.reshape(seq_count, block_len, width_here),
            ],
            axis=2,
        ),
        "ctx",
        axis=1,
        tiled=True,
    )
    key_tags = lax.all_gather(block_ids, "ctx", axis=1, tiled=True)
    key_heads = key_value[:, :, :width_here].reshape(seq_count, seq_len, heads_here, HD)
    value_heads = key_value[:, :, width_here:].reshape(seq_count, seq_len, heads_here, HD)
    logits = (
        jnp.einsum("sqhd,skhd->shqk", query_rot, key_heads, preferred_element_type=jnp.float32)
        * score_scale
        - score_shift
    )
    allowed = key_tags[:, None, None, :] <= block_ids[:, None, :, None]
    squashed = jax.nn.sigmoid(logits)
    weights = jnp.where(allowed, squashed, 0.0).astype(low)
    attended = jnp.einsum(
        "shqk,skhd->sqhd", weights, value_heads, preferred_element_type=jnp.float32
    )
    mixed_rows = attended.reshape(row_count, width_here).astype(low)
    attend_part = sum_rows(plain_dot(mixed_rows, output_full))
    middle = token_part + attend_part
    scale_two = inverse_rms(middle)
    normed_two = every_row((middle * scale_two * gain_two).astype(low))
    gate_vals = plain_dot(normed_two, gate_full)
    up_vals = plain_dot(normed_two, up_full)
    gate_sig = jax.nn.sigmoid(gate_vals)
    gate_act = gate_vals * gate_sig
    hidden = (gate_act * up_vals).astype(low)
    grad_hidden = dot_last(grad_rows, down_full)
    slope = gate_sig * (1.0 + gate_vals * (1.0 - gate_sig))
    grad_gate = (grad_hidden * up_vals * slope).astype(low)
    grad_up = (grad_hidden * gate_act).astype(low)
    grad_normed_two = sum_rows(dot_last(grad_gate, gate_full) + dot_last(grad_up, up_full))
    feed_part = sum_rows(plain_dot(hidden, down_full))
    result = middle + feed_part
    layer_out = every_row(result.astype(low)).reshape(tokens.shape)
    grad_middle_norm, grad_gain_two = norm_back(grad_normed_two, middle, scale_two, gain_two)
    grad_middle = cotangent_part + grad_middle_norm
    grad_attend = every_row(grad_middle.astype(low))

    def scatter(value, dimension):
        return lax.psum_scatter(
            value.astype(low), ("fsdp", "ctx"), scatter_dimension=dimension, tiled=True
        ).astype(jnp.float32)

    grad_down = scatter(dot_first(hidden, grad_rows), 1)
    grad_gate_w = scatter(dot_first(normed_two, grad_gate), 0)
    grad_up_w = scatter(dot_first(normed_two, grad_up), 0)
    grad_mixed = dot_last(grad_attend, output_full).astype(low)
    grad_output_w = scatter(dot_first(mixed_rows, grad_attend), 1)
    grad_mixed_heads = grad_mixed.reshape(shape_heads)
    grad_weights = jnp.einsum(
        "sqhd,skhd->shqk", grad_mixed_heads, value_heads, preferred_element_type=jnp.float32
    )
    grad_logits = jnp.where(allowed, grad_weights * squashed * (1.0 - squashed), 0.0).astype(low)
    grad_query = score_scale * jnp.einsum(
        "shqk,skhd->sqhd", grad_logits, key_heads, preferred_element_type=jnp.float32
    )
    key_part = score_scale * jnp.einsum(
        "shqk,sqhd->skhd", grad_logits, query_rot, preferred_element_type=jnp.float32
    )
    value_part = jnp.einsum(
        "shqk,sqhd->skhd", weights, grad_mixed_heads, preferred_element_type=jnp.float32
    )
    pair = jnp.concatenate(
        [
            key_part.reshape(seq_count, seq_len, width_here).astype(low),
            value_part.reshape(seq_count, seq_len, width_here).astype(low),
        ],
        axis=2,
    )
    mine = lax.psum_scatter(pair, "ctx", scatter_dimension=1, tiled=True).astype(jnp.float32)
    grad_query_rows = rotate(grad_query, cosine, sine_table, -1.0).reshape(row_count, width_here)
    grad_key_rows = rotate(
        mine[:, :, :width_here].reshape(shape_heads), cosine, sine_table, -1.0
    ).reshape(row_count, width_here)
    grad_qkv = jnp.concatenate(
        [
            grad_query_rows.astype(low),
            grad_key_rows.astype(low),
            mine[:, :, width_here:].reshape(row_count, width_here).astype(low),
        ],
        axis=1,
    )
    grad_normed_one = sum_rows(dot_last(grad_qkv, qkv_full))
    grad_qkv_w = scatter(dot_first(normed_one, grad_qkv), 0)
    scale_one_part = lax.dynamic_slice_in_dim(scale_one, row_at, part_rows, 0)
    grad_input_norm, grad_gain_one = norm_back(
        grad_normed_one, token_part, scale_one_part, gain_one
    )
    grad_input = every_row((grad_middle + grad_input_norm).astype(low)).reshape(tokens.shape)
    sums = jnp.stack(
        [
            jnp.sum(result * result),
            jnp.sum(attend_part * attend_part),
            jnp.sum(feed_part * feed_part),
        ]
    )
    small = lax.psum(jnp.concatenate([grad_gain_one, grad_gain_two, sums]), ("fsdp", "ctx", "tp"))
    shards = lax.axis_size("fsdp") * ctx_size
    entries = float(row_count * model_width * shards)
    roots = jnp.sqrt(small[2 * model_width :] / entries)
    gain_part = model_width // shards
    gain_at = (lax.axis_index("fsdp") * ctx_size + lax.axis_index("ctx")) * gain_part
    grad_gain_attend = lax.dynamic_slice_in_dim(small, gain_at, gain_part, 0)
    grad_gain_feed = lax.dynamic_slice_in_dim(small, model_width + gain_at, gain_part, 0)
    return (
        layer_out,
        grad_input,
        grad_gain_attend,
        grad_qkv_w[:, :width_here],
        grad_qkv_w[:, width_here : 2 * width_here],
        grad_qkv_w[:, 2 * width_here :],
        grad_output_w,
        grad_gain_feed,
        grad_gate_w,
        grad_up_w,
        grad_down,
        roots[0],
        roots[1],
        roots[2],
    )


def solution(mesh):
    placed = (
        P("fsdp", "ctx", None),
        P("fsdp", "ctx"),
        P("fsdp", "ctx"),
        P("fsdp"),
        P("fsdp", "tp"),
        P("fsdp", "tp"),
        P("fsdp", "tp"),
        P("tp", "fsdp"),
        P("fsdp"),
        P("fsdp", "tp"),
        P("fsdp", "tp"),
        P("tp", "fsdp"),
        P("fsdp", "ctx", None),
    )
    return jax.shard_map(
        local,
        mesh=mesh,
        in_specs=placed,
        out_specs=(
            P("fsdp", "ctx", None),
            P("fsdp", "ctx", None),
            P(("fsdp", "ctx")),
            P(("fsdp", "ctx"), "tp"),
            P(("fsdp", "ctx"), "tp"),
            P(("fsdp", "ctx"), "tp"),
            P("tp", ("fsdp", "ctx")),
            P(("fsdp", "ctx")),
            P(("fsdp", "ctx"), "tp"),
            P(("fsdp", "ctx"), "tp"),
            P("tp", ("fsdp", "ctx")),
            P(),
            P(),
            P(),
        ),
        check_vma=False,
    )
```

profile of v0, /device:TPU:0, one launch (start us, length us, event | category | flops | bytes accessed | tf_op | source)
XLA Modules:
  0.0 1552.7 jit_solution(17306718815725621846)
XLA Ops:
  21.3 37.3 %all-gather.11.cloned.1.call-done = bf16[2048,1536]{1,0:T(8,128)(2,1)} async-done(((bf16[256,1536]{1,0:T(8,128)(2,1)}), bf16[2048,1536]{1,0:T(8,128)(2,1)}) %all-gather.11.cloned.1.call-update) | async-done | bytes 6291472 | tf_op jit(solution)/shard_map/all_gather | solution.py:67
  99.7 50.8 %all-gather.13.cloned.1.call-done = bf16[4,1024,1024]{1,2,0:T(8,128)(2,1)} async-done(((bf16[4,256,1024]{1,2,0:T(8,128)(2,1)}), bf16[4,1024,1024]{1,2,0:T(8,128)(2,1)}) %all-gather.13.cloned.1.call-update) | async-done | bytes 8388624 | tf_op jit(solution)/shard_map/all_gather | solution.py:139
  186.8 72.2 %reduce-scatter.11.cloned.1.call-done = bf16[256,2048]{1,0:T(8,128)(2,1)} async-done(((bf16[1024,2048]{1,0:T(8,128)(2,1)}), bf16[256,2048]{1,0:T(8,128)(2,1)}) %reduce-scatter.11.cloned.1.call-update) | async-done | bytes 1048592 | tf_op jit(solution)/shard_map/reduce_scatter | solution.py:80
  266.7 48.8 %all-gather.23.cloned.1.call-done = bf16[4096,1024]{1,0:T(8,128)(2,1)} async-done(((bf16[512,1024]{1,0:T(8,128)(2,1)}), bf16[4096,1024]{1,0:T(8,128)(2,1)}) %all-gather.23.cloned.1.call-update) | async-done | bytes 8388624 | tf_op jit(solution)/shard_map/all_gather | solution.py:73
  315.5 11.9 copy.67
  327.4 44.1 %all-gather.21.cloned.1.call-done = bf16[2048,2048]{1,0:T(8,128)(2,1)} async-done(((bf16[256,2048]{1,0:T(8,128)(2,1)}), bf16[2048,2048]{1,0:T(8,128)(2,1)}) %all-gather.21.cloned.1.call-update) | async-done | bytes 8388624 | tf_op jit(solution)/shard_map/all_gather | solution.py:67
  371.6 82.9 %all-gather.17.cloned.1.call-done = bf16[1024,2048]{1,0:T(8,128)(2,1)} async-done(((bf16[256,2048]{1,0:T(8,128)(2,1)}), bf16[1024,2048]{1,0:T(8,128)(2,1)}) %all-gather.17.cloned.1.call-update) | async-done | bytes 4194320 | tf_op jit(solution)/shard_map/all_gather | solution.py:86
  454.5 14.6 fusion.50
  469.0 40.7 %all-gather.19.cloned.1.call-done = bf16[2048,2048]{1,0:T(8,128)(2,1)} async-done(((bf16[256,2048]{1,0:T(8,128)(2,1)}), bf16[2048,2048]{1,0:T(8,128)(2,1)}) %all-gather.19.cloned.1.call-update) | async-done | bytes 8388624 | tf_op jit(solution)/shard_map/all_gather | solution.py:67
  509.7 14.7 fusion.49
  524.4 19.1 %fusion.2 = (bf16[1024,2048]{1,0:T(8,128)(2,1)}, bf16[1024,2048]{1,0:T(8,128)(2,1)}, bf16[1024,2048]{1,0:T(8,128)(2,1)}) fusion(f32[1024,2048]{1,0:T(8,128)} %fusion.49, f32[1024,2048]{1,0:T(8,128)} %fusion.50, bf16[1024,2048]{1,0:T(8,128)(2,1)S(1)} %bitcast.143, bf16[2048,2048]{0,1:T(8,128)(2,1)} %bitcast.121), kind=kOutput, calls=%fused_computation.8 | convolution fusion | flops 8621391872 | bytes 41943040 | tf_op jit(solution)/shard_map/dot_general | solution.py:17
  543.5 12.9 fusion.51
  556.4 12.9 add_convert_fusion
  569.3 14.0 convolution_convert_fusion.5
  583.6 62.6 %reduce-scatter.15.cloned.1.call-done = bf16[256,2048]{1,0:T(8,128)(2,1)} async-done(((bf16[1024,2048]{1,0:T(8,128)(2,1)}), bf16[256,2048]{1,0:T(8,128)(2,1)}) %reduce-scatter.15.cloned.1.call-update) | async-done | bytes 1048592 | tf_op jit(solution)/shard_map/reduce_scatter | solution.py:80
  646.2 79.4 %reduce-scatter.13.cloned.1.call-done = bf16[256,2048]{1,0:T(8,128)(2,1)} async-done(((bf16[1024,2048]{1,0:T(8,128)(2,1)}), bf16[256,2048]{1,0:T(8,128)(2,1)}) %reduce-scatter.13.cloned.1.call-update) | async-done | bytes 1048592 | tf_op jit(solution)/shard_map/reduce_scatter | solution.py:80
  734.2 81.4 %all-gather.27.cloned.1.call-done = bf16[1024,2048]{1,0:T(8,128)(2,1)} async-done(((bf16[256,2048]{1,0:T(8,128)(2,1)}), bf16[1024,2048]{1,0:T(8,128)(2,1)}) %all-gather.27.cloned.1.call-update) | async-done | bytes 4194320 | tf_op jit(solution)/shard_map/all_gather | solution.py:86
  835.7 12.9 convolution_convert_fusion.8
  870.4 61.7 %reduce-scatter.17.cloned.1.call-done = bf16[4,256,1024]{1,2,0:T(8,128)(2,1)} async-done(((bf16[4,1024,1024]{1,2,0:T(8,128)(2,1)}), bf16[4,256,1024]{1,2,0:T(8,128)(2,1)}) %reduce-scatter.17.cloned.1.call-update) | async-done | bytes 2097168 | tf_op jit(solution)/shard_map/reduce_scatter | solution.py:218
  962.7 14.1 convolution_convert_fusion
  976.9 14.2 convolution_convert_fusion.1
  991.4 14.0 convolution_convert_fusion.2
  1012.6 11.2 convolution_convert_fusion.3
  1024.5 14.9 reduce-scatter.19.cloned.1.call-done
  1046.4 68.2 %reduce-scatter.29.cloned.1.call-done = bf16[2048,256]{1,0:T(8,128)(2,1)} async-done(((bf16[2048,2048]{1,0:T(8,128)(2,1)}), bf16[2048,256]{1,0:T(8,128)(2,1)}) %reduce-scatter.29.cloned.1.call-update) | async-done | bytes 1048592 | tf_op jit(solution)/shard_map/reduce_scatter | solution.py:188
  1117.3 72.1 %reduce-scatter.27.cloned.1.call-done = bf16[256,2048]{1,0:T(8,128)(2,1)} async-done(((bf16[2048,2048]{1,0:T(8,128)(2,1)}), bf16[256,2048]{1,0:T(8,128)(2,1)}) %reduce-scatter.27.cloned.1.call-update) | async-done | bytes 1048592 | tf_op jit(solution)/shard_map/reduce_scatter | solution.py:188
  1192.2 72.0 %reduce-scatter.25.cloned.1.call-done = bf16[256,2048]{1,0:T(8,128)(2,1)} async-done(((bf16[2048,2048]{1,0:T(8,128)(2,1)}), bf16[256,2048]{1,0:T(8,128)(2,1)}) %reduce-scatter.25.cloned.1.call-update) | async-done | bytes 1048592 | tf_op jit(solution)/shard_map/reduce_scatter | solution.py:188
  1267.1 79.4 %all-gather.25.cloned.1.call-done = bf16[1024,2048]{1,0:T(8,128)(2,1)} async-done(((bf16[256,2048]{1,0:T(8,128)(2,1)}), bf16[1024,2048]{1,0:T(8,128)(2,1)}) %all-gather.25.cloned.1.call-update) | async-done | bytes 4194320 | tf_op jit(solution)/shard_map/all_gather | solution.py:86
  1346.5 43.4 %reduce-scatter.23.cloned.1.call-done = bf16[512,256]{1,0:T(8,128)(2,1)} async-done(((bf16[512,2048]{1,0:T(8,128)(2,1)}), bf16[512,256]{1,0:T(8,128)(2,1)}) %reduce-scatter.23.cloned.1.call-update) | async-done | bytes 262160 | tf_op jit(solution)/shard_map/reduce_scatter | solution.py:188
  1393.6 40.0 %psum.7 = f32[4099]{0:T(1024)S(1)} all-reduce(f32[4099]{0:T(1024)S(1)} %concatenate.39), channel_id=1, replica_groups=mesh['fsdp'=2,'ctx'=4,'tp'=4] {'fsdp','ctx','tp'}, use_global_device_ids=true, to_apply=%region_14.15 | all-reduce | flops 4099 | bytes 32792 | tf_op jit(solution)/shard_map/psum | solution.py:245
  1434.8 20.8 %reduce-scatter.21.cloned.1.call-done = bf16[256,1536]{1,0:T(8,128)(2,1)} async-done(((bf16[2048,1536]{1,0:T(8,128)(2,1)}), bf16[256,1536]{1,0:T(8,128)(2,1)}) %reduce-scatter.21.cloned.1.call-update) | async-done | bytes 786448 | tf_op jit(solution)/shard_map/reduce_scatter | solution.py:188
  1458.0 80.4 %all-gather.29.cloned.1.call-done = bf16[1024,2048]{1,0:T(8,128)(2,1)} async-done(((bf16[256,2048]{1,0:T(8,128)(2,1)}), bf16[1024,2048]{1,0:T(8,128)(2,1)}) %all-gather.29.cloned.1.call-update) | async-done | bytes 4194320 | tf_op jit(solution)/shard_map/all_gather | solution.py:86
  (180 shorter events, 217.7 us)
Async XLA Ops:
  7.2 51.4 %all-gather.11.cloned.1.call-start = ((), (), s32[]{:S(2)}) async-start(), calls=%async_computation.10 | async-start | bytes 7077888 | tf_op jit(solution)/shard_map/all_gather | solution.py:67
  9.4 86.2 %all-gather.15.cloned.1.call-start = ((), (), s32[]{:S(2)}) async-start(), calls=%async_computation.12 | async-start | bytes 2359296 | tf_op jit(solution)/shard_map/all_gather | solution.py:73
  10.2 140.2 %all-gather.13.cloned.1.call-start = ((), (), s32[]{:S(2)}) async-start(), calls=%async_computation.11 | async-start | bytes 10485760 | tf_op jit(solution)/shard_map/all_gather | solution.py:139
  19.4 49.4 %copy-start.23 = (f32[1,2,4,128]{3,1,2,0:T(2,128)}, f32[1,2,4,128]{3,1,2,0:T(2,128)S(1)}, u32[]{:S(2)}) copy-start(f32[1,2,4,128]{3,1,2,0:T(2,128)S(1)} %copy.90) | copy-start | bytes 12292
  19.4 49.4 %copy-start.18 = (f32[1,2048]{1,0:T(1,128)}, f32[1,2048]{1,0:T(1,128)S(1)}, u32[]{:S(2)}) copy-start(f32[1,2048]{1,0:T(1,128)S(1)} %get-tuple-element.57) | copy-start | bytes 24580
  21.3 62.8 %copy-start.7 = (f32[4,256,64]{2,1,0:T(8,128)}, f32[4,256,64]{2,1,0:T(8,128)S(1)}, u32[]{:S(2)}) copy-start(f32[4,256,64]{2,1,0:T(8,128)S(1)} %get-tuple-element.58) | copy-start | bytes 786436
  21.3 62.8 %copy-start.8 = (f32[4,256,64]{2,1,0:T(8,128)}, f32[4,256,64]{2,1,0:T(8,128)S(1)}, u32[]{:S(2)}) copy-start(f32[4,256,64]{2,1,0:T(8,128)S(1)} %get-tuple-element.59) | copy-start | bytes 786436
  89.5 169.5 %reduce-scatter.11.cloned.1.call-start = ((), (), s32[]{:S(2)}) async-start(), calls=%async_computation.13 | async-start | bytes 5242880 | tf_op jit(solution)/shard_map/reduce_scatter | solution.py:80
  99.6 56.1 %copy-start.9 = (bf16[4,256,4,64]{3,1,2,0:T(8,128)(2,1)S(1)}, bf16[4,256,4,64]{3,1,2,0:T(8,128)(2,1)}, u32[]{:S(2)}) copy-start(bf16[4,256,4,64]{3,1,2,0:T(8,128)(2,1)} %get-tuple-element.32) | copy-start | bytes 1572868
  155.8 8.5 copy-start.4
  182.0 133.5 %all-gather.23.cloned.1.call-start = ((), (), s32[]{:S(2)}) async-start(), calls=%async_computation.17 | async-start | bytes 9437184 | tf_op jit(solution)/shard_map/all_gather | solution.py:73
  184.4 187.2 %all-gather.21.cloned.1.call-start = ((), (), s32[]{:S(2)}) async-start(), calls=%async_computation.16 | async-start | bytes 9437184 | tf_op jit(solution)/shard_map/all_gather | solution.py:67
  186.8 267.7 %all-gather.17.cloned.1.call-start = ((), (), s32[]{:S(2)}) async-start(), calls=%async_computation.14 | async-start | bytes 5242880 | tf_op jit(solution)/shard_map/all_gather | solution.py:86
  263.9 245.8 %all-gather.19.cloned.1.call-start = ((), (), s32[]{:S(2)}) async-start(), calls=%async_computation.15 | async-start | bytes 9437184 | tf_op jit(solution)/shard_map/all_gather | solution.py:67
  266.3 379.9 %reduce-scatter.15.cloned.1.call-start = ((), (), s32[]{:S(2)}) async-start(), calls=%async_computation.20 | async-start | bytes 5242880 | tf_op jit(solution)/shard_map/reduce_scatter | solution.py:80
  509.7 14.7 copy-start.17
  543.5 12.9 copy-start.27
  569.3 156.4 %reduce-scatter.13.cloned.1.call-start = ((), (), s32[]{:S(2)}) async-start(), calls=%async_computation.18 | async-start | bytes 5242880 | tf_op jit(solution)/shard_map/reduce_scatter | solution.py:80
  583.3 142.4 %copy-start.3 = (bf16[256,2048]{1,0:T(8,128)(2,1)S(1)}, bf16[256,2048]{1,0:T(8,128)(2,1)}, u32[]{:S(2)}) copy-start(bf16[256,2048]{1,0:T(8,128)(2,1)} %reduce-scatter.11.cloned.1.call-done) | copy-start | bytes 3145732
  583.3 232.3 %all-gather.27.cloned.1.call-start = ((), (), s32[]{:S(2)}) async-start(), calls=%async_computation.21 | async-start | bytes 5242880 | tf_op jit(solution)/shard_map/all_gather | solution.py:86
  734.2 197.9 %reduce-scatter.17.cloned.1.call-start = ((), (), s32[]{:S(2)}) async-start(), calls=%async_computation.22 | async-start | bytes 10485760 | tf_op jit(solution)/shard_map/reduce_scatter | solution.py:218
  835.6 12.9 copy-start.2
  862.2 177.2 %reduce-scatter.19.cloned.1.call-start = ((), (), s32[]{:S(2)}) async-start(), calls=%async_computation.23 | async-start | bytes 5242880 | tf_op jit(solution)/shard_map/reduce_scatter | solution.py:80
  946.5 7.8 slice-start
  962.5 152.1 %reduce-scatter.29.cloned.1.call-start = ((), (), s32[]{:S(2)}) async-start(), calls=%async_computation.29 | async-start | bytes 9437184 | tf_op jit(solution)/shard_map/reduce_scatter | solution.py:188
  976.8 212.6 %reduce-scatter.27.cloned.1.call-start = ((), (), s32[]{:S(2)}) async-start(), calls=%async_computation.28 | async-start | bytes 9437184 | tf_op jit(solution)/shard_map/reduce_scatter | solution.py:188
  991.1 273.2 %reduce-scatter.25.cloned.1.call-start = ((), (), s32[]{:S(2)}) async-start(), calls=%async_computation.27 | async-start | bytes 9437184 | tf_op jit(solution)/shard_map/reduce_scatter | solution.py:188
  1005.4 341.0 %all-gather.25.cloned.1.call-start = ((), (), s32[]{:S(2)}) async-start(), calls=%async_computation.19 | async-start | bytes 5242880 | tf_op jit(solution)/shard_map/all_gather | solution.py:86
  1006.0 383.8 %reduce-scatter.23.cloned.1.call-start = ((), (), s32[]{:S(2)}) async-start(), calls=%async_computation.26 | async-start | bytes 2359296 | tf_op jit(solution)/shard_map/reduce_scatter | solution.py:188
  1012.5 443.1 %reduce-scatter.21.cloned.1.call-start = ((), (), s32[]{:S(2)}) async-start(), calls=%async_computation.25 | async-start | bytes 7077888 | tf_op jit(solution)/shard_map/reduce_scatter | solution.py:188
  1023.9 18.2 %copy-start.6 = (bf16[256,2048]{1,0:T(8,128)(2,1)S(1)}, bf16[256,2048]{1,0:T(8,128)(2,1)}, u32[]{:S(2)}) copy-start(bf16[256,2048]{1,0:T(8,128)(2,1)} %reduce-scatter.15.cloned.1.call-done) | copy-start | bytes 3145732
  1023.9 514.6 %all-gather.29.cloned.1.call-start = ((), (), s32[]{:S(2)}) async-start(), calls=%async_computation.24 | async-start | bytes 5242880 | tf_op jit(solution)/shard_map/all_gather | solution.py:86
  (18 other events, 61.8 us)
Sparse Core Ops, SparseCore 0:
  10.5 48.1 all-gather.10
  61.1 27.7 all-gather.14
  91.1 59.3 all-gather.12
  182.2 76.7 reduce-scatter.10
  260.7 54.7 all-gather.22
  317.3 54.2 all-gather.20
  373.7 80.7 all-gather.16
  456.9 52.7 all-gather.18
  569.4 76.7 reduce-scatter.14
  648.3 77.2 reduce-scatter.12
  734.3 81.2 all-gather.26
  862.3 69.7 reduce-scatter.16
  962.6 76.7 reduce-scatter.18
  1042.8 71.7 reduce-scatter.28
  1117.9 71.4 reduce-scatter.26
  1192.7 71.4 reduce-scatter.24
  1265.7 80.7 all-gather.24
  1350.2 39.6 reduce-scatter.22
  1393.2 62.4 reduce-scatter.20
  1457.7 80.7 all-gather.28
where the time goes:
time: 1560 us; the launch traced here: 1550 us
  waiting for transfers between devices  1110 us (71%)
  matrix products  233 us (15%)
  local copies, waits for them, and re-layouts  81.4 us (5%)
  other arithmetic  55.9 us (4%)
  blocking collectives  50.7 us (3%)
    all_gather x4, waiting for transfers between devices, every_row(): return lax.all_gather(rows, 'tp', axis=0, tiled=True)  324 us
    reduce_scatter x5, waiting for transfers between devices, scatter(): lax.psum_scatter(value.astype(low), ('fsdp', 'ctx'), scatter_dimension=di...  277 us
    reduce_scatter x4, waiting for transfers between devices, sum_rows(): lax.psum_scatter(partial.astype(jnp.bfloat16), 'tp', scatter_dimension=0,...  229 us
    all_gather x3, waiting for transfers between devices, spread_rows(): return lax.all_gather(mine, ('fsdp', 'ctx'), axis=0, tiled=True)  122 us
    reduce_scatter x1, waiting for transfers between devices, local(): lax.psum_scatter(pair, 'ctx', scatter_dimension=1, tiled=True)  61.7 us
    dot_general x5, matrix products, plain_dot(): return jnp.dot(left_side, right_side, preferred_element_type=jnp.float32)  59.6 us
    dot_general x5, matrix products, dot_first(): lax.dot_general(left_side, right_side, (((0,), (0,)), ((), ())), preferre...  59.5 us
    dot_general x5, matrix products, dot_last(): lax.dot_general(left_side, right_side, (((1,), (1,)), ((), ())), preferre...  59.2 us
  transfers between devices with their start and end apart: 20, of which 19 were waited for; matrix products, arithmetic and copies ran while one was open for 12% of the time, Pallas kernels for 0%

commit v1 on v0

--- a/solution.py
+++ b/solution.py
@@ -242,7 +242,12 @@
             jnp.sum(feed_part * feed_part),
         ]
     )
-    small = lax.psum(jnp.concatenate([grad_gain_one, grad_gain_two, sums]), ("fsdp", "ctx", "tp"))
+    small = jnp.sum(
+        lax.all_gather(
+            jnp.concatenate([grad_gain_one, grad_gain_two, sums]), ("fsdp", "ctx", "tp")
+        ),
+        axis=0,
+    )
     shards = lax.axis_size("fsdp") * ctx_size
     entries = float(row_count * model_width * shards)
     roots = jnp.sqrt(small[2 * model_width :] / entries)

time: 1560 us -> 1680 us (1.077)
  waiting for transfers between devices: 1110 us -> 1270 us
  blocking collectives: 50.7 us -> 10.7 us
    unnamed x20 -> x22, waiting for transfers between devices: 0.84 us -> 132 us
    psum x1 -> x0, blocking collectives: 40 us -> none  [local(): lax.psum(jnp.concatenate([grad_gain_one, grad_gain_two, sums]), ('fsdp',...]
    reduce_scatter x5, waiting for transfers between devices: 277 us -> 303 us  [scatter(): lax.psum_scatter(value.astype(low), ('fsdp', 'ctx'), scatter_dimension=di...]
  transfers between devices with their start and end apart: 20 -> 21, of which waited for: 19 -> 20; matrix products, arithmetic and copies ran while one was open for 12% -> 12% of each run, Pallas kernels for 0% -> 0%
where the time goes in v1:
time: 1680 us; the launch traced here: 1670 us
  waiting for transfers between devices  1270 us (76%)
  matrix products  235 us (14%)
  local copies, waits for them, and re-layouts  81.1 us (5%)
  other arithmetic  55.6 us (3%)
    all_gather x4, waiting for transfers between devices, every_row(): return lax.all_gather(rows, 'tp', axis=0, tiled=True)  324 us
    reduce_scatter x5, waiting for transfers between devices, scatter(): lax.psum_scatter(value.astype(low), ('fsdp', 'ctx'), scatter_dimension=di...  303 us
    reduce_scatter x4, waiting for transfers between devices, sum_rows(): lax.psum_scatter(partial.astype(jnp.bfloat16), 'tp', scatter_dimension=0,...  229 us
    unnamed x22, waiting for transfers between devices  132 us
    all_gather x3, waiting for transfers between devices, spread_rows(): return lax.all_gather(mine, ('fsdp', 'ctx'), axis=0, tiled=True)  122 us
    reduce_scatter x1, waiting for transfers between devices, local(): lax.psum_scatter(pair, 'ctx', scatter_dimension=1, tiled=True)  61.7 us
    dot_general x5, matrix products, dot_last(): lax.dot_general(left_side, right_side, (((1,), (1,)), ((), ())), preferre...  61.5 us
    dot_general x5, matrix products, plain_dot(): return jnp.dot(left_side, right_side, preferred_element_type=jnp.float32)  59.8 us
  transfers between devices with their start and end apart: 21, of which 20 were waited for; matrix products, arithmetic and copies ran while one was open for 12% of the time, Pallas kernels for 0%

profile of v1, /device:TPU:0, one launch (start us, length us, event | category | flops | bytes accessed | tf_op | source)
XLA Modules:
  0.0 1673.9 jit_solution(3732665813783324318)
XLA Ops:
  21.3 37.3 %all-gather.12.cloned.1.call-done = bf16[2048,1536]{1,0:T(8,128)(2,1)} async-done(((bf16[256,1536]{1,0:T(8,128)(2,1)}), bf16[2048,1536]{1,0:T(8,128)(2,1)}) %all-gather.12.cloned.1.call-update) | async-done | bytes 6291472 | tf_op jit(solution)/shard_map/all_gather | solution.py:67
  98.0 52.5 %all-gather.14.cloned.1.call-done = bf16[4,1024,1024]{1,2,0:T(8,128)(2,1)} async-done(((bf16[4,256,1024]{1,2,0:T(8,128)(2,1)}), bf16[4,1024,1024]{1,2,0:T(8,128)(2,1)}) %all-gather.14.cloned.1.call-update) | async-done | bytes 8388624 | tf_op jit(solution)/shard_map/all_gather | solution.py:139
  186.8 72.1 %reduce-scatter.11.cloned.1.call-done = bf16[256,2048]{1,0:T(8,128)(2,1)} async-done(((bf16[1024,2048]{1,0:T(8,128)(2,1)}), bf16[256,2048]{1,0:T(8,128)(2,1)}) %reduce-scatter.11.cloned.1.call-update) | async-done | bytes 1048592 | tf_op jit(solution)/shard_map/reduce_scatter | solution.py:80
  266.7 48.8 %all-gather.24.cloned.1.call-done = bf16[4096,1024]{1,0:T(8,128)(2,1)} async-done(((bf16[512,1024]{1,0:T(8,128)(2,1)}), bf16[4096,1024]{1,0:T(8,128)(2,1)}) %all-gather.24.cloned.1.call-update) | async-done | bytes 8388624 | tf_op jit(solution)/shard_map/all_gather | solution.py:73
  315.5 11.9 copy.88
  327.4 44.1 %all-gather.22.cloned.1.call-done = bf16[2048,2048]{1,0:T(8,128)(2,1)} async-done(((bf16[256,2048]{1,0:T(8,128)(2,1)}), bf16[2048,2048]{1,0:T(8,128)(2,1)}) %all-gather.22.cloned.1.call-update) | async-done | bytes 8388624 | tf_op jit(solution)/shard_map/all_gather | solution.py:67
  371.5 82.9 %all-gather.18.cloned.1.call-done = bf16[1024,2048]{1,0:T(8,128)(2,1)} async-done(((bf16[256,2048]{1,0:T(8,128)(2,1)}), bf16[1024,2048]{1,0:T(8,128)(2,1)}) %all-gather.18.cloned.1.call-update) | async-done | bytes 4194320 | tf_op jit(solution)/shard_map/all_gather | solution.py:86
  454.4 14.6 fusion.50
  469.0 40.7 %all-gather.20.cloned.1.call-done = bf16[2048,2048]{1,0:T(8,128)(2,1)} async-done(((bf16[256,2048]{1,0:T(8,128)(2,1)}), bf16[2048,2048]{1,0:T(8,128)(2,1)}) %all-gather.20.cloned.1.call-update) | async-done | bytes 8388624 | tf_op jit(solution)/shard_map/all_gather | solution.py:67
  509.7 14.7 fusion.49
  524.4 19.1 %fusion.2 = (bf16[1024,2048]{1,0:T(8,128)(2,1)}, bf16[1024,2048]{1,0:T(8,128)(2,1)}, bf16[1024,2048]{1,0:T(8,128)(2,1)}) fusion(f32[1024,2048]{1,0:T(8,128)} %fusion.49, f32[1024,2048]{1,0:T(8,128)} %fusion.50, bf16[1024,2048]{1,0:T(8,128)(2,1)S(1)} %bitcast.143, bf16[2048,2048]{0,1:T(8,128)(2,1)} %bitcast.121), kind=kOutput, calls=%fused_computation.8 | convolution fusion | flops 8621391872 | bytes 41943040 | tf_op jit(solution)/shard_map/dot_general | solution.py:17
  543.4 14.1 convolution_convert_fusion.5
  557.6 12.7 fusion.51
  570.4 12.9 add_convert_fusion
  583.5 51.0 %reduce-scatter.13.cloned.1.call-done = bf16[256,2048]{1,0:T(8,128)(2,1)} async-done(((bf16[1024,2048]{1,0:T(8,128)(2,1)}), bf16[256,2048]{1,0:T(8,128)(2,1)}) %reduce-scatter.13.cloned.1.call-update) | async-done | bytes 1048592 | tf_op jit(solution)/shard_map/reduce_scatter | solution.py:80
  634.5 79.4 %reduce-scatter.15.cloned.1.call-done = bf16[256,2048]{1,0:T(8,128)(2,1)} async-done(((bf16[1024,2048]{1,0:T(8,128)(2,1)}), bf16[256,2048]{1,0:T(8,128)(2,1)}) %reduce-scatter.15.cloned.1.call-update) | async-done | bytes 1048592 | tf_op jit(solution)/shard_map/reduce_scatter | solution.py:80
  722.5 81.4 %all-gather.28.cloned.1.call-done = bf16[1024,2048]{1,0:T(8,128)(2,1)} async-done(((bf16[256,2048]{1,0:T(8,128)(2,1)}), bf16[1024,2048]{1,0:T(8,128)(2,1)}) %all-gather.28.cloned.1.call-update) | async-done | bytes 4194320 | tf_op jit(solution)/shard_map/all_gather | solution.py:86
  824.0 12.9 convolution_convert_fusion.8
  858.7 61.7 %reduce-scatter.17.cloned.1.call-done = bf16[4,256,1024]{1,2,0:T(8,128)(2,1)} async-done(((bf16[4,1024,1024]{1,2,0:T(8,128)(2,1)}), bf16[4,256,1024]{1,2,0:T(8,128)(2,1)}) %reduce-scatter.17.cloned.1.call-update) | async-done | bytes 2097168 | tf_op jit(solution)/shard_map/reduce_scatter | solution.py:218
  950.8 14.1 convolution_convert_fusion.2
  965.0 14.1 convolution_convert_fusion.1
  979.4 14.1 convolution_convert_fusion
  1000.8 26.7 %reduce-scatter.19.cloned.1.call-done = bf16[256,2048]{1,0:T(8,128)(2,1)} async-done(((bf16[1024,2048]{1,0:T(8,128)(2,1)}), bf16[256,2048]{1,0:T(8,128)(2,1)}) %reduce-scatter.19.cloned.1.call-update) | async-done | bytes 1048592 | tf_op jit(solution)/shard_map/reduce_scatter | solution.py:80
  1033.5 11.3 convolution_convert_fusion.3
  1050.8 52.0 %reduce-scatter.25.cloned.1.call-done = bf16[256,2048]{1,0:T(8,128)(2,1)} async-done(((bf16[2048,2048]{1,0:T(8,128)(2,1)}), bf16[256,2048]{1,0:T(8,128)(2,1)}) %reduce-scatter.25.cloned.1.call-update) | async-done | bytes 1048592 | tf_op jit(solution)/shard_map/reduce_scatter | solution.py:188
  1105.7 72.0 %reduce-scatter.27.cloned.1.call-done = bf16[256,2048]{1,0:T(8,128)(2,1)} async-done(((bf16[2048,2048]{1,0:T(8,128)(2,1)}), bf16[256,2048]{1,0:T(8,128)(2,1)}) %reduce-scatter.27.cloned.1.call-update) | async-done | bytes 1048592 | tf_op jit(solution)/shard_map/reduce_scatter | solution.py:188
  1180.5 71.8 %reduce-scatter.29.cloned.1.call-done = bf16[2048,256]{1,0:T(8,128)(2,1)} async-done(((bf16[2048,2048]{1,0:T(8,128)(2,1)}), bf16[2048,256]{1,0:T(8,128)(2,1)}) %reduce-scatter.29.cloned.1.call-update) | async-done | bytes 1048592 | tf_op jit(solution)/shard_map/reduce_scatter | solution.py:188
  1255.0 79.5 %all-gather.26.cloned.1.call-done = bf16[1024,2048]{1,0:T(8,128)(2,1)} async-done(((bf16[256,2048]{1,0:T(8,128)(2,1)}), bf16[1024,2048]{1,0:T(8,128)(2,1)}) %all-gather.26.cloned.1.call-update) | async-done | bytes 4194320 | tf_op jit(solution)/shard_map/all_gather | solution.py:86
  1334.5 43.4 %reduce-scatter.23.cloned.1.call-done = bf16[512,256]{1,0:T(8,128)(2,1)} async-done(((bf16[512,2048]{1,0:T(8,128)(2,1)}), bf16[512,256]{1,0:T(8,128)(2,1)}) %reduce-scatter.23.cloned.1.call-update) | async-done | bytes 262160 | tf_op jit(solution)/shard_map/reduce_scatter | solution.py:188
  1379.6 131.1 %all-reduce.3.cloned.1.call-done = f32[131168]{0:T(1024)} async-done(((f32[131168]{0:T(1024)}), f32[131168]{0:T(1024)}) %all-reduce.3.cloned.1.call-update) | async-done | bytes 524688
  1513.5 63.3 %reduce-scatter.21.cloned.1.call-done = bf16[256,1536]{1,0:T(8,128)(2,1)} async-done(((bf16[2048,1536]{1,0:T(8,128)(2,1)}), bf16[256,1536]{1,0:T(8,128)(2,1)}) %reduce-scatter.21.cloned.1.call-update) | async-done | bytes 786448 | tf_op jit(solution)/shard_map/reduce_scatter | solution.py:188
  1579.1 80.6 %all-gather.30.cloned.1.call-done = bf16[1024,2048]{1,0:T(8,128)(2,1)} async-done(((bf16[256,2048]{1,0:T(8,128)(2,1)}), bf16[1024,2048]{1,0:T(8,128)(2,1)}) %all-gather.30.cloned.1.call-update) | async-done | bytes 4194320 | tf_op jit(solution)/shard_map/all_gather | solution.py:86
  (181 shorter events, 219.5 us)
Async XLA Ops:
  7.2 51.4 %all-gather.12.cloned.1.call-start = ((), (), s32[]{:S(2)}) async-start(), calls=%async_computation.10 | async-start | bytes 7077888 | tf_op jit(solution)/shard_map/all_gather | solution.py:67
  9.4 84.5 %all-gather.16.cloned.1.call-start = ((), (), s32[]{:S(2)}) async-start(), calls=%async_computation.12 | async-start | bytes 2359296 | tf_op jit(solution)/shard_map/all_gather | solution.py:73
  10.2 140.2 %all-gather.14.cloned.1.call-start = ((), (), s32[]{:S(2)}) async-start(), calls=%async_computation.11 | async-start | bytes 10485760 | tf_op jit(solution)/shard_map/all_gather | solution.py:139
  15.7 53.1 %copy-start.18 = (f32[1,2048]{1,0:T(1,128)}, f32[1,2048]{1,0:T(1,128)S(1)}, u32[]{:S(2)}) copy-start(f32[1,2048]{1,0:T(1,128)S(1)} %get-tuple-element.57) | copy-start | bytes 24580
  19.4 49.4 %copy-start.23 = (f32[1,2,4,128]{3,1,2,0:T(2,128)}, f32[1,2,4,128]{3,1,2,0:T(2,128)S(1)}, u32[]{:S(2)}) copy-start(f32[1,2,4,128]{3,1,2,0:T(2,128)S(1)} %copy.111) | copy-start | bytes 12292
  21.3 60.6 %copy-start.7 = (f32[4,256,64]{2,1,0:T(8,128)}, f32[4,256,64]{2,1,0:T(8,128)S(1)}, u32[]{:S(2)}) copy-start(f32[4,256,64]{2,1,0:T(8,128)S(1)} %get-tuple-element.58) | copy-start | bytes 786436
  21.3 60.6 %copy-start.8 = (f32[4,256,64]{2,1,0:T(8,128)}, f32[4,256,64]{2,1,0:T(8,128)S(1)}, u32[]{:S(2)}) copy-start(f32[4,256,64]{2,1,0:T(8,128)S(1)} %get-tuple-element.59) | copy-start | bytes 786436
  87.8 171.1 %reduce-scatter.11.cloned.1.call-start = ((), (), s32[]{:S(2)}) async-start(), calls=%async_computation.13 | async-start | bytes 5242880 | tf_op jit(solution)/shard_map/reduce_scatter | solution.py:80
  97.9 57.8 %copy-start.9 = (bf16[4,256,4,64]{3,1,2,0:T(8,128)(2,1)S(1)}, bf16[4,256,4,64]{3,1,2,0:T(8,128)(2,1)}, u32[]{:S(2)}) copy-start(bf16[4,256,4,64]{3,1,2,0:T(8,128)(2,1)} %get-tuple-element.32) | copy-start | bytes 1572868
  182.0 133.5 %all-gather.24.cloned.1.call-start = ((), (), s32[]{:S(2)}) async-start(), calls=%async_computation.17 | async-start | bytes 9437184 | tf_op jit(solution)/shard_map/all_gather | solution.py:73
  184.4 187.2 %all-gather.22.cloned.1.call-start = ((), (), s32[]{:S(2)}) async-start(), calls=%async_computation.16 | async-start | bytes 9437184 | tf_op jit(solution)/shard_map/all_gather | solution.py:67
  186.8 267.7 %all-gather.18.cloned.1.call-start = ((), (), s32[]{:S(2)}) async-start(), calls=%async_computation.14 | async-start | bytes 5242880 | tf_op jit(solution)/shard_map/all_gather | solution.py:86
  263.8 245.8 %all-gather.20.cloned.1.call-start = ((), (), s32[]{:S(2)}) async-start(), calls=%async_computation.15 | async-start | bytes 9437184 | tf_op jit(solution)/shard_map/all_gather | solution.py:67
  266.2 368.3 %reduce-scatter.13.cloned.1.call-start = ((), (), s32[]{:S(2)}) async-start(), calls=%async_computation.18 | async-start | bytes 5242880 | tf_op jit(solution)/shard_map/reduce_scatter | solution.py:80
  509.7 14.7 copy-start.17
  557.6 156.4 %reduce-scatter.15.cloned.1.call-start = ((), (), s32[]{:S(2)}) async-start(), calls=%async_computation.20 | async-start | bytes 5242880 | tf_op jit(solution)/shard_map/reduce_scatter | solution.py:80
  557.6 12.7 copy-start.27
  583.2 130.7 %copy-start.3 = (bf16[256,2048]{1,0:T(8,128)(2,1)S(1)}, bf16[256,2048]{1,0:T(8,128)(2,1)}, u32[]{:S(2)}) copy-start(bf16[256,2048]{1,0:T(8,128)(2,1)} %reduce-scatter.11.cloned.1.call-done) | copy-start | bytes 3145732
  583.3 220.6 %all-gather.28.cloned.1.call-start = ((), (), s32[]{:S(2)}) async-start(), calls=%async_computation.21 | async-start | bytes 5242880 | tf_op jit(solution)/shard_map/all_gather | solution.py:86
  722.5 197.9 %reduce-scatter.17.cloned.1.call-start = ((), (), s32[]{:S(2)}) async-start(), calls=%async_computation.22 | async-start | bytes 10485760 | tf_op jit(solution)/shard_map/reduce_scatter | solution.py:218
  824.0 12.9 copy-start.2
  850.5 177.0 %reduce-scatter.19.cloned.1.call-start = ((), (), s32[]{:S(2)}) async-start(), calls=%async_computation.23 | async-start | bytes 5242880 | tf_op jit(solution)/shard_map/reduce_scatter | solution.py:80
  950.6 152.3 %reduce-scatter.25.cloned.1.call-start = ((), (), s32[]{:S(2)}) async-start(), calls=%async_computation.27 | async-start | bytes 9437184 | tf_op jit(solution)/shard_map/reduce_scatter | solution.py:188
  964.9 212.8 %reduce-scatter.27.cloned.1.call-start = ((), (), s32[]{:S(2)}) async-start(), calls=%async_computation.28 | async-start | bytes 9437184 | tf_op jit(solution)/shard_map/reduce_scatter | solution.py:188
  979.1 273.2 %reduce-scatter.29.cloned.1.call-start = ((), (), s32[]{:S(2)}) async-start(), calls=%async_computation.29 | async-start | bytes 9437184 | tf_op jit(solution)/shard_map/reduce_scatter | solution.py:188
  993.5 341.0 %all-gather.26.cloned.1.call-start = ((), (), s32[]{:S(2)}) async-start(), calls=%async_computation.19 | async-start | bytes 5242880 | tf_op jit(solution)/shard_map/all_gather | solution.py:86
  994.1 33.4 %copy-start.19 = (f32[1,2048]{1,0:T(1,128)S(1)}, f32[1,2048]{1,0:T(1,128)}, u32[]{:S(2)}) copy-start(f32[1,2048]{1,0:T(1,128)} %copy-done.18) | copy-start | bytes 24580
  994.2 383.7 %reduce-scatter.23.cloned.1.call-start = ((), (), s32[]{:S(2)}) async-start(), calls=%async_computation.26 | async-start | bytes 2359296 | tf_op jit(solution)/shard_map/reduce_scatter | solution.py:188
  1000.6 32.8 %copy-start.24 = (f32[1,2,4,128]{3,1,2,0:T(2,128)S(1)}, f32[1,2,4,128]{3,1,2,0:T(2,128)}, u32[]{:S(2)}) copy-start(f32[1,2,4,128]{3,1,2,0:T(2,128)} %copy-done.23) | copy-start | bytes 12292
  1000.7 510.1 %all-reduce.3.cloned.1.call-start = ((), (), s32[]{:S(2)}) async-start(), calls=%async_computation.30 | async-start | bytes 1056768
  1033.4 543.3 %reduce-scatter.21.cloned.1.call-start = ((), (), s32[]{:S(2)}) async-start(), calls=%async_computation.25 | async-start | bytes 7077888 | tf_op jit(solution)/shard_map/reduce_scatter | solution.py:188
  1044.8 614.8 %all-gather.30.cloned.1.call-start = ((), (), s32[]{:S(2)}) async-start(), calls=%async_computation.24 | async-start | bytes 5242880 | tf_op jit(solution)/shard_map/all_gather | solution.py:86
  (17 other events, 69.2 us)
Sparse Core Ops, SparseCore 0:
  10.5 48.1 all-gather.11
  61.1 27.7 all-gather.15
  91.0 59.3 all-gather.13
  182.1 76.7 reduce-scatter.10
  260.7 54.7 all-gather.23
  317.2 54.2 all-gather.21
  373.7 80.7 all-gather.17
  456.9 52.7 all-gather.19
  557.7 76.7 reduce-scatter.12
  636.7 77.2 reduce-scatter.14
  722.6 81.2 all-gather.27
  850.6 69.7 reduce-scatter.16
  950.7 76.7 reduce-scatter.18
  1030.8 72.0 reduce-scatter.24
  1106.2 71.4 reduce-scatter.26
  1181.0 71.2 reduce-scatter.28
  1253.7 80.7 all-gather.25
  1338.2 39.6 reduce-scatter.22
  1383.1 127.6 all-reduce.2
  1514.0 62.6 reduce-scatter.20
  1578.9 80.7 all-gather.29
